TPU v7x, 128 devices: a whole 4x4x4 slice. The times are simulated.
128 devices in a mesh: dp: 8 (over x, z_hi), tp: 16 (over z_lo, y, core).
Axes of the slice: x: 4, y: 4, z: 4 (z_hi: 2, z_lo: 2; z = z_hi * 2 + z_lo), core: 2. Of those that a mesh axis runs over, the one named last changes fastest.
Arguments:
- hidden_in: bfloat16 [4, 64, 4096], P(None, 'dp'), may hold values from -6 to 6
- pre_gain: float32 [4096], replicated, may hold values from 0.25 to 1.75
- w_zx: bfloat16 [4096, 2, 8192], P(None, None, 'tp'), may hold values from -0.09375 to 0.09375
- zx_codes: bfloat16 [4096, 2, 8192], P(('dp', 'tp')), may hold values from -4 to 4
- zx_exponents: int32 [32, 2, 64], P('dp', None, 'tp'), may hold values from -9 to -6
- w_bc: bfloat16 [4096, 2048], P(None, 'tp'), may hold values from -0.09375 to 0.09375
- w_dt: bfloat16 [4096, 128], P(None, 'tp'), may hold values from -0.09375 to 0.09375
- conv_x: float32 [5, 8192], P(None, 'tp'), may hold values from -0.6 to 0.6
- conv_bc: float32 [5, 2048], P(None, 'tp'), may hold values from -0.6 to 0.6
- dt_bias: float32 [128], P('tp'), may hold values from -2 to 0.5
- decay_rate: float32 [128], P('tp'), may hold values from 0.05 to 2
- skip_gain: float32 [128], P('tp'), may hold values from 0.5 to 1.5
- conv_state_x: bfloat16 [64, 3, 8192], P('dp', None, 'tp'), may hold values from -6 to 6
- conv_state_bc: bfloat16 [64, 3, 2048], P('dp', None, 'tp'), may hold values from -6 to 6
- ssm_state: float32 [64, 128, 64, 256], P('dp', 'tp'), may hold values from -6 to 6
- norm_gain: float32 [8192], P('tp'), may hold values from 0.25 to 1.75
- w_out: bfloat16 [8192, 4096], P('tp'), may hold values from -0.0625 to 0.0625
- out_codes: bfloat16 [8192, 4096], P('tp', 'dp'), may hold values from -4 to 4
- out_exponents: int32 [64, 32], P('tp', 'dp'), may hold values from -7 to -4
Outputs:
- mixed: bfloat16 [4, 64, 4096], P(None, 'dp', 'tp')
- final_state: float32 [64, 128, 64, 256], P('dp', 'tp')
All inputs are finite; a program needn't handle non-finite values.
Results may differ from a plain program's by a relative error of at most 0.014.
Values may be sent and summed in bfloat16 or wider, within the bound.
No kernel may reach another device: no remote copies, remote signals or barrier semaphores. Data moves between devices by JAX's collectives and lax.ppermute only.
A program may use at most 128 MiB of HBM per device.

v0:
```python
import jax
import jax.numpy as jnp
from jax import lax
from jax.sharding import PartitionSpec as P

H = 128
G = 4
BLK = 128
STEPS = 4
DI = 8192
EPS = 1e-05


def joined_along(tiles, dim):
    lengths = list(tiles.shape[1:])
    lengths[dim] *= tiles.shape[0]
    return jnp.moveaxis(tiles, 0, dim).reshape(lengths)


def copy_for_each(value, axis):
    devices = lax.axis_size(axis)
    return lax.all_to_all(
        jnp.broadcast_to(value[None], (devices, *value.shape)), axis, 0, 0, tiled=True
    )


def gather_directly(value, axis, dim):
    return joined_along(copy_for_each(value, axis), dim)


def cut_along(value, dim, devices):
    before, after = (value.shape[:dim], value.shape[dim + 1 :])
    return jnp.moveaxis(value.reshape(*before, devices, -1, *after), dim, 0)


def sent_and_summed(value, axis, dim):
    devices = lax.axis_size(axis)
    tiles = lax.all_to_all(cut_along(value, dim, devices), axis, 0, 0, tiled=True)
    return jnp.sum(tiles, axis=0)


def of_everyone(value, axis):
    return copy_for_each(value, axis).sum(axis=0)


def decode_pairs(codes, exponents, block):
    rows, pair, cols = codes.shape
    blocked = codes.astype(jnp.float32).reshape(rows // block, block, pair, cols // block, block)
    scales = jnp.exp2(exponents.astype(jnp.float32))
    return (blocked * scales[:, None, :, :, None]).reshape(rows, pair, cols)


def decode_matrix(codes, exponents, block):
    rows, cols = codes.shape
    blocked = codes.astype(jnp.float32).reshape(rows // block, block, cols // block, block)
    scales = jnp.exp2(exponents.astype(jnp.float32))
    return (blocked * scales[:, None, :, None]).reshape(rows, cols)


def conv_step(history, fresh, params):
    window = jnp.concatenate([history, fresh[:, None, :]], axis=1)
    mixed = jnp.sum(window * params[:4][None], axis=1) + params[4]
    return (jax.nn.silu(mixed), window[:, 1:])


def body(
    hidden_in,
    pre_gain,
    w_zx,
    zx_codes,
    zx_exponents,
    w_bc,
    w_dt,
    conv_x,
    conv_bc,
    dt_bias,
    decay_rate,
    skip_gain,
    conv_state_x,
    conv_state_bc,
    ssm_state,
    norm_gain,
    w_out,
    out_codes,
    out_exponents,
):
    replica = lax.axis_index("dp")
    slot = lax.axis_index("tp")
    traded = lax.all_to_all(zx_codes, "tp", split_axis=2, concat_axis=0, tiled=True)
    zx_delta = decode_pairs(traded, zx_exponents, BLK)
    row_span = traded.shape[0]
    local_cols = traded.shape[2]
    w_rows = lax.dynamic_slice_in_dim(w_zx, replica * row_span, row_span, 0)
    zx_weights = (
        (w_rows.astype(jnp.float32) + zx_delta)
        .astype(jnp.bfloat16)
        .reshape(row_span, 2 * local_cols)
    )
    out_piece = decode_matrix(out_codes, out_exponents, BLK).astype(jnp.bfloat16)
    out_full = lax.all_gather(out_piece, "dp", axis=1, tiled=True)
    new_out = (w_out.astype(jnp.float32) + out_full.astype(jnp.float32)).astype(jnp.bfloat16)
    heads_here = ssm_state.shape[1]
    states_n = ssm_state.shape[3]
    group = slot * heads_here // (H // G)
    group_mask = (jnp.arange(G) == group).astype(jnp.float32)
    history_x = conv_state_x.astype(jnp.float32)
    history_bc = conv_state_bc.astype(jnp.float32)
    state = ssm_state
    results = []
    carried = None
    for step in range(STEPS):
        x = hidden_in[step].astype(jnp.float32)
        if step > 0:
            x = x + carried.astype(jnp.float32)
        rows = x.shape[0]
        normed = (x * lax.rsqrt(jnp.mean(x * x, -1, keepdims=True) + EPS) * pre_gain).astype(
            jnp.bfloat16
        )
        everyone = gather_directly(normed, "dp", 0)
        own_cols = lax.dynamic_slice_in_dim(everyone, replica * row_span, row_span, 1)
        zx = sent_and_summed(
            jnp.dot(own_cols, zx_weights, preferred_element_type=jnp.float32), "dp", 0
        )
        zx = zx.reshape(rows, 2, local_cols)
        gate = zx[:, 0]
        inner = zx[:, 1]
        bc_raw = jnp.dot(normed, w_bc, preferred_element_type=jnp.float32)
        dt_raw = jnp.dot(normed, w_dt, preferred_element_type=jnp.float32)
        conv_inner, history_x = conv_step(history_x, inner, conv_x)
        conv_piece, history_bc = conv_step(history_bc, bc_raw, conv_bc)
        bc_all = gather_directly(conv_piece, "tp", 1)
        b_group = lax.dynamic_slice_in_dim(bc_all, group * states_n, states_n, 1)
        c_group = lax.dynamic_slice_in_dim(bc_all, G * states_n + group * states_n, states_n, 1)
        step_size = jax.nn.softplus(dt_raw + dt_bias)
        decay = jnp.exp(-step_size * decay_rate)
        inner_heads = conv_inner.reshape(rows, heads_here, -1)
        state = (
            decay[:, :, None, None] * state
            + (step_size[:, :, None] * inner_heads)[:, :, :, None] * b_group[:, None, None, :]
        )
        read = (
            jnp.einsum("rhpn,rn->rhp", state, c_group, precision=lax.Precision.HIGHEST)
            + skip_gain[:, None] * inner_heads
        )
        gated = read.reshape(rows, local_cols) * jax.nn.silu(gate)
        squares = jnp.sum(gated * gated, -1)
        totals = of_everyone(squares[:, None] * group_mask, "tp")
        mean_sq = jnp.sum(totals * group_mask, -1) / (DI // G)
        scaled = (gated * lax.rsqrt(mean_sq + EPS)[:, None] * norm_gain).astype(jnp.bfloat16)
        partial_value = jnp.dot(scaled, new_out, preferred_element_type=jnp.float32)
        summed = sent_and_summed(partial_value, "tp", 1).astype(jnp.bfloat16)
        results.append(summed)
        if step + 1 < STEPS:
            carried = gather_directly(summed, "tp", 1)
    return (jnp.stack(results), state)


def solution(mesh):
    return jax.shard_map(
        body,
        mesh=mesh,
        in_specs=(
            P(None, "dp", None),
            P(),
            P(None, None, "tp"),
            P(("dp", "tp"), None, None),
            P("dp", None, "tp"),
            P(None, "tp"),
            P(None, "tp"),
            P(None, "tp"),
            P(None, "tp"),
            P("tp"),
            P("tp"),
            P("tp"),
            P("dp", None, "tp"),
            P("dp", None, "tp"),
            P("dp", "tp", None, None),
            P("tp"),
            P("tp", None),
            P("tp", "dp"),
            P("tp", "dp"),
        ),
        out_specs=(P(None, "dp", "tp"), P("dp", "tp", None, None)),
        check_vma=False,
    )
```

profile of v0, /device:TPU:1, one launch (start us, length us, event | category | flops | bytes accessed | tf_op | source)
XLA Modules:
  0.0 413.4 jit_solution(10557720529095760822)
XLA Ops:
  10.4 7.4 %copy.32 = bf16[32,2,8192]{0,1,2:T(2,128)(2,1)} copy(bf16[32,2,8192]{2,1,0:T(2,128)(2,1)S(1)} %copy-done.4) | data formatting | bytes 2097152 | tf_op args[3]
  17.8 10.0 %reshape.669 = bf16[16,2,16384]{2,1,0:T(2,128)(2,1)} reshape(bf16[8192,2,32]{2,1,0:T(2,128)(2,1)} %bitcast.196) | data formatting | bytes 2097152
  27.8 7.3 %all-to-all-start.1 = ((bf16[16,2,16384]{2,1,0:T(2,128)(2,1)}), bf16[16,2,16384]{2,1,0:T(2,128)(2,1)S(1)}, u32[]{:S(2)}, u32[]{:S(2)}) async-start(bf16[16,2,16384]{2,1,0:T(2,128)(2,1)} %reshape.669), calls=%async_computation.1 | async-start | bytes 2097152 | tf_op jit(solution)/shard_map/all_to_all | solution.py:89
  42.1 8.8 %all-to-all-done.1 = bf16[16,2,16384]{2,1,0:T(2,128)(2,1)S(1)} async-done(((bf16[16,2,16384]{2,1,0:T(2,128)(2,1)}), bf16[16,2,16384]{2,1,0:T(2,128)(2,1)S(1)}, u32[]{:S(2)}, u32[]{:S(2)}) %all-to-all-start.1) | async-done | bytes 1048608 | tf_op jit(solution)/shard_map/all_to_all | solution.py:89
  51.7 7.0 %all-to-all-start = ((bf16[8,8,4096]{2,1,0:T(8,128)(2,1)}), bf16[8,8,4096]{2,1,0:T(8,128)(2,1)}, u32[]{:S(2)}, u32[]{:S(2)}) async-start(bf16[8,8,4096]{2,1,0:T(8,128)(2,1)} %broadcast_in_dim.47), calls=%async_computation | async-start | bytes 1048576 | tf_op jit(solution)/shard_map/all_to_all | solution.py:22
  62.2 8.9 %convert_bitcast_fusion = f32[16,32,2,512]{1,2,3,0:T(2,128)} fusion(bf16[32,2,16,512]{0,1,3,2:T(2,128)(2,1)} %bitcast.195), kind=kLoop, calls=%fused_computation | loop fusion | flops 524288 | bytes 3145728 | tf_op jit(solution)/shard_map/convert_element_type | solution.py:48
  71.1 11.6 %copy.33 = f32[16,32,2,512]{3,2,1,0:T(2,128)} copy(f32[16,32,2,512]{1,2,3,0:T(2,128)} %convert_bitcast_fusion) | data formatting | bytes 4194304 | tf_op jit(solution)/shard_map/convert_element_type | solution.py:48
  98.4 6.9 %all-to-all-start.2 = ((f32[8,8,1024]{2,1,0:T(8,128)}), f32[8,8,1024]{2,1,0:T(8,128)S(1)}, u32[]{:S(2)}, u32[]{:S(2)}) async-start(f32[8,8,1024]{2,1,0:T(8,128)} %fusion.49), calls=%async_computation.2 | async-start | bytes 524288 | tf_op jit(solution)/shard_map/all_to_all | solution.py:38
  113.7 7.6 %fusion.1 = f32[8,1,8,64]{3,1,2,0:T(1,128)S(1)} fusion(f32[8,8,64,256]{3,2,1,0:T(8,128)} %param.33, f32[8,256]{1,0:T(8,128)S(1)} %get-tuple-element.17, f32[8,8,64]{2,1,0:T(8,128)S(1)} %broadcast_multiply_fusion.3, f32[8,8]{1,0:T(8,128)S(1)} %get-tuple-element.26, f32[8,256,1,1]{1,0,2,3:T(8,128)S(1)} %get-tuple-element.16), kind=kOutput, calls=%fused_computation.7 | convolution fusion | flops 15728640 | bytes 4243712 | tf_op jit(solution)/shard_map/rhpn,rn->rhp/dot_general | solution.py:142
  133.7 7.3 %fusion = bf16[4096,512]{0,1:T(8,128)(2,1)} fusion(bf16[512,4096]{1,0:T(8,128)(2,1)} %all-gather.2.cloned.1.call-done, bf16[512,4096]{1,0:T(8,128)(2,1)} %param.35), kind=kLoop, calls=%fused_computation.2 | loop fusion | flops 8388608 | bytes 12582912 | tf_op jit(solution)/shard_map/dot_general | solution.py:150
  141.0 6.5 %copy.46 = bf16[4096,512]{1,0:T(8,128)(2,1)} copy(bf16[4096,512]{0,1:T(8,128)(2,1)} %fusion) | data formatting | bytes 8388608 | tf_op jit(solution)/shard_map/dot_general | solution.py:150
  176.8 10.2 %all-to-all-done.7 = bf16[8,8,4096]{2,1,0:T(8,128)(2,1)S(1)} async-done(((bf16[8,8,4096]{2,1,0:T(8,128)(2,1)}), bf16[8,8,4096]{2,1,0:T(8,128)(2,1)S(1)}, u32[]{:S(2)}, u32[]{:S(2)}) %all-to-all-start.7) | async-done | bytes 524320 | tf_op jit(solution)/shard_map/all_to_all | solution.py:22
  201.6 7.2 %all-to-all-done.8 = f32[8,8,1024]{2,1,0:T(8,128)S(1)} async-done(((f32[8,8,1024]{2,1,0:T(8,128)}), f32[8,8,1024]{2,1,0:T(8,128)S(1)}, u32[]{:S(2)}, u32[]{:S(2)}) %all-to-all-start.8) | async-done | bytes 262176 | tf_op jit(solution)/shard_map/all_to_all | solution.py:38
  209.1 7.6 %fusion.11 = f32[8,1,8,64]{3,1,2,0:T(1,128)S(1)} fusion(f32[8,8,64,256]{3,2,1,0:T(8,128)} %param.33, f32[8,256]{1,0:T(8,128)S(1)} %get-tuple-element.15, f32[8,8,64]{2,1,0:T(8,128)S(1)} %broadcast_multiply_fusion.2, f32[8,8]{1,0:T(8,128)S(1)} %get-tuple-element.28, f32[8,256]{1,0:T(8,128)S(1)} %get-tuple-element.17, ...), kind=kOutput, calls=%fused_computation.22 | convolution fusion | flops 18874368 | bytes 4268544 | tf_op jit(solution)/shard_map/rhpn,rn->rhp/dot_general | solution.py:142
  217.0 10.2 %all_to_all.124 = f32[16,8,4]{1,2,0:T(4,128)S(1)} all-to-all(f32[16,8,4]{1,2,0:T(4,128)S(1)} %broadcast_in_dim.56), channel_id=1, replica_groups=mesh['dp'=8,'tp'=16] {'tp'}, dimensions={0} | all-to-all | bytes 4096 | tf_op jit(solution)/shard_map/all_to_all | solution.py:22
  256.7 10.4 %all-to-all-done.13 = bf16[8,8,4096]{2,1,0:T(8,128)(2,1)S(1)} async-done(((bf16[8,8,4096]{2,1,0:T(8,128)(2,1)}), bf16[8,8,4096]{2,1,0:T(8,128)(2,1)S(1)}, u32[]{:S(2)}, u32[]{:S(2)}) %all-to-all-start.13) | async-done | bytes 524320 | tf_op jit(solution)/shard_map/all_to_all | solution.py:22
  281.7 7.4 %all-to-all-done.14 = f32[8,8,1024]{2,1,0:T(8,128)S(1)} async-done(((f32[8,8,1024]{2,1,0:T(8,128)}), f32[8,8,1024]{2,1,0:T(8,128)S(1)}, u32[]{:S(2)}, u32[]{:S(2)}) %all-to-all-start.14) | async-done | bytes 262176 | tf_op jit(solution)/shard_map/all_to_all | solution.py:38
  289.3 8.0 %fusion.2 = f32[8,1,8,64]{3,1,2,0:T(1,128)S(1)} fusion(f32[8,256]{1,0:T(8,128)S(1)} %get-tuple-element.13, f32[8,8,64]{2,1,0:T(8,128)S(1)} %broadcast_multiply_fusion.1, f32[8,8]{1,0:T(8,128)S(1)} %get-tuple-element.30, f32[8,8,64,256]{3,2,1,0:T(8,128)} %param.33, f32[8,256]{1,0:T(8,128)S(1)} %get-tuple-element.15, ...), kind=kOutput, calls=%fused_computation.8 | convolution fusion | flops 22020096 | bytes 4293376 | tf_op jit(solution)/shard_map/rhpn,rn->rhp/dot_general | solution.py:142
  297.6 10.0 %all_to_all.125 = f32[16,8,4]{1,2,0:T(4,128)S(1)} all-to-all(f32[16,8,4]{1,2,0:T(4,128)S(1)} %broadcast_in_dim.62), channel_id=1, replica_groups=mesh['dp'=8,'tp'=16] {'tp'}, dimensions={0} | all-to-all | bytes 4096 | tf_op jit(solution)/shard_map/all_to_all | solution.py:22
  337.2 10.4 %all-to-all-done.19 = bf16[8,8,4096]{2,1,0:T(8,128)(2,1)S(1)} async-done(((bf16[8,8,4096]{2,1,0:T(8,128)(2,1)}), bf16[8,8,4096]{2,1,0:T(8,128)(2,1)S(1)}, u32[]{:S(2)}, u32[]{:S(2)}) %all-to-all-start.19) | async-done | bytes 524320 | tf_op jit(solution)/shard_map/all_to_all | solution.py:22
  362.1 7.4 %all-to-all-done.20 = f32[8,8,1024]{2,1,0:T(8,128)S(1)} async-done(((f32[8,8,1024]{2,1,0:T(8,128)}), f32[8,8,1024]{2,1,0:T(8,128)S(1)}, u32[]{:S(2)}, u32[]{:S(2)}) %all-to-all-start.20) | async-done | bytes 262176 | tf_op jit(solution)/shard_map/all_to_all | solution.py:38
  369.8 6.2 %multiply_add_fusion = f32[8,8,64,256]{3,2,1,0:T(8,128)S(1)} fusion(f32[8,256]{1,0:T(8,128)S(1)} %get-tuple-element.11, f32[8,8,64]{2,1,0:T(8,128)S(1)} %broadcast_multiply_fusion, f32[8,8]{1,0:T(8,128)S(1)} %get-tuple-element.32, f32[8,256]{1,0:T(8,128)S(1)} %get-tuple-element.13, f32[8,8,64]{2,1,0:T(8,128)S(1)} %broadcast_multiply_fusion.1, ...), kind=kLoop, calls=%fused_computation.3 | loop fusion | flops 12582912 | bytes 8487936 | tf_op jit(solution)/shard_map/add | solution.py:138
  383.3 10.0 %all_to_all.126 = f32[16,8,4]{1,2,0:T(4,128)S(1)} all-to-all(f32[16,8,4]{1,2,0:T(4,128)S(1)} %broadcast_in_dim.68), channel_id=1, replica_groups=mesh['dp'=8,'tp'=16] {'tp'}, dimensions={0} | all-to-all | bytes 4096 | tf_op jit(solution)/shard_map/all_to_all | solution.py:22
  397.0 8.9 %all_to_all.127 = f32[16,8,256]{2,1,0:T(8,128)S(1)} all-to-all(f32[16,8,256]{2,1,0:T(8,128)S(1)} %convolution_bitcast_fusion), channel_id=1, replica_groups=mesh['dp'=8,'tp'=16] {'tp'}, dimensions={0} | all-to-all | bytes 262144 | tf_op jit(solution)/shard_map/all_to_all | solution.py:38
  (206 shorter events, 195.5 us)
Async XLA Ops:
  7.2 126.6 %all-gather.2.cloned.1.call-start = ((), (), s32[]{:S(2)}) async-start(), calls=%async_computation.24 | async-start | bytes 4718592 | tf_op jit(solution)/shard_map/all_gather | solution.py:100
  27.8 23.1 %all-to-all-start.1 = ((bf16[16,2,16384]{2,1,0:T(2,128)(2,1)}), bf16[16,2,16384]{2,1,0:T(2,128)(2,1)S(1)}, u32[]{:S(2)}, u32[]{:S(2)}) async-start(bf16[16,2,16384]{2,1,0:T(2,128)(2,1)} %reshape.669), calls=%async_computation.1 | async-start | bytes 2097152 | tf_op jit(solution)/shard_map/all_to_all | solution.py:89
  51.7 35.9 %all-to-all-start = ((bf16[8,8,4096]{2,1,0:T(8,128)(2,1)}), bf16[8,8,4096]{2,1,0:T(8,128)(2,1)}, u32[]{:S(2)}, u32[]{:S(2)}) async-start(bf16[8,8,4096]{2,1,0:T(8,128)(2,1)} %broadcast_in_dim.47), calls=%async_computation | async-start | bytes 1048576 | tf_op jit(solution)/shard_map/all_to_all | solution.py:22
  86.8 34.5 %copy-start.7 = (f32[8]{0:T(128)S(1)}, f32[8]{0:T(128)}, u32[]{:S(2)}) copy-start(f32[8]{0:T(128)} %param.30) | copy-start | bytes 100
  87.6 40.0 %copy-start.13 = (f32[512]{0:T(512)S(1)}, f32[512]{0:T(512)}, u32[]{:S(2)}) copy-start(f32[512]{0:T(512)} %param.34) | copy-start | bytes 6148
  88.2 10.2 %all-to-all-start.3 = ((f32[16,8,128]{2,1,0:T(8,128)}), f32[16,8,128]{2,1,0:T(8,128)S(1)}, u32[]{:S(2)}, u32[]{:S(2)}) async-start(f32[16,8,128]{2,1,0:T(8,128)} %broadcast_in_dim.49), calls=%async_computation.3 | async-start | bytes 131072 | tf_op jit(solution)/shard_map/all_to_all | solution.py:22
  98.4 14.3 %all-to-all-start.2 = ((f32[8,8,1024]{2,1,0:T(8,128)}), f32[8,8,1024]{2,1,0:T(8,128)S(1)}, u32[]{:S(2)}, u32[]{:S(2)}) async-start(f32[8,8,1024]{2,1,0:T(8,128)} %fusion.49), calls=%async_computation.2 | async-start | bytes 524288 | tf_op jit(solution)/shard_map/all_to_all | solution.py:38
  122.3 11.2 %all-to-all-start.4 = ((f32[16,8,4]{1,2,0:T(4,128)}), f32[16,8,4]{1,2,0:T(4,128)S(1)}, u32[]{:S(2)}, u32[]{:S(2)}) async-start(f32[16,8,4]{1,2,0:T(4,128)} %broadcast_in_dim.50), calls=%async_computation.4 | async-start | bytes 65536 | tf_op jit(solution)/shard_map/all_to_all | solution.py:22
  151.5 49.9 %copy-start.11 = (f32[8]{0:T(128)S(1)}, f32[8]{0:T(128)}, u32[]{:S(2)}) copy-start(f32[8]{0:T(128)} %param.28) | copy-start | bytes 100
  151.5 10.0 %all-to-all-start.5 = ((f32[16,8,256]{2,1,0:T(8,128)}), f32[16,8,256]{2,1,0:T(8,128)S(1)}, u32[]{:S(2)}, u32[]{:S(2)}) async-start(f32[16,8,256]{2,1,0:T(8,128)} %convolution_bitcast_fusion.3), calls=%async_computation.5 | async-start | bytes 262144 | tf_op jit(solution)/shard_map/all_to_all | solution.py:38
  162.1 9.7 %all-to-all-start.6 = ((bf16[16,8,256]{2,1,0:T(8,128)(2,1)}), bf16[16,8,256]{2,1,0:T(8,128)(2,1)S(1)}, u32[]{:S(2)}, u32[]{:S(2)}) async-start(bf16[16,8,256]{2,1,0:T(8,128)(2,1)} %broadcast_in_dim.51), calls=%async_computation.6 | async-start | bytes 131072 | tf_op jit(solution)/shard_map/all_to_all | solution.py:22
  173.0 14.0 %all-to-all-start.7 = ((bf16[8,8,4096]{2,1,0:T(8,128)(2,1)}), bf16[8,8,4096]{2,1,0:T(8,128)(2,1)S(1)}, u32[]{:S(2)}, u32[]{:S(2)}) async-start(bf16[8,8,4096]{2,1,0:T(8,128)(2,1)} %broadcast_in_dim.53), calls=%async_computation.7 | async-start | bytes 1048576 | tf_op jit(solution)/shard_map/all_to_all | solution.py:22
  187.7 10.3 %all-to-all-start.9 = ((f32[16,8,128]{2,1,0:T(8,128)}), f32[16,8,128]{2,1,0:T(8,128)S(1)}, u32[]{:S(2)}, u32[]{:S(2)}) async-start(f32[16,8,128]{2,1,0:T(8,128)} %broadcast_in_dim.55), calls=%async_computation.9 | async-start | bytes 131072 | tf_op jit(solution)/shard_map/all_to_all | solution.py:22
  198.0 10.8 %all-to-all-start.8 = ((f32[8,8,1024]{2,1,0:T(8,128)}), f32[8,8,1024]{2,1,0:T(8,128)S(1)}, u32[]{:S(2)}, u32[]{:S(2)}) async-start(f32[8,8,1024]{2,1,0:T(8,128)} %fusion.47), calls=%async_computation.8 | async-start | bytes 524288 | tf_op jit(solution)/shard_map/all_to_all | solution.py:38
  231.6 9.8 %all-to-all-start.11 = ((f32[16,8,256]{2,1,0:T(8,128)}), f32[16,8,256]{2,1,0:T(8,128)S(1)}, u32[]{:S(2)}, u32[]{:S(2)}) async-start(f32[16,8,256]{2,1,0:T(8,128)} %convolution_bitcast_fusion.2), calls=%async_computation.11 | async-start | bytes 262144 | tf_op jit(solution)/shard_map/all_to_all | solution.py:38
  242.0 9.7 %all-to-all-start.12 = ((bf16[16,8,256]{2,1,0:T(8,128)(2,1)}), bf16[16,8,256]{2,1,0:T(8,128)(2,1)S(1)}, u32[]{:S(2)}, u32[]{:S(2)}) async-start(bf16[16,8,256]{2,1,0:T(8,128)(2,1)} %broadcast_in_dim.57), calls=%async_computation.12 | async-start | bytes 131072 | tf_op jit(solution)/shard_map/all_to_all | solution.py:22
  253.0 14.2 %all-to-all-start.13 = ((bf16[8,8,4096]{2,1,0:T(8,128)(2,1)}), bf16[8,8,4096]{2,1,0:T(8,128)(2,1)S(1)}, u32[]{:S(2)}, u32[]{:S(2)}) async-start(bf16[8,8,4096]{2,1,0:T(8,128)(2,1)} %broadcast_in_dim.59), calls=%async_computation.13 | async-start | bytes 1048576 | tf_op jit(solution)/shard_map/all_to_all | solution.py:22
  267.8 10.3 %all-to-all-start.15 = ((f32[16,8,128]{2,1,0:T(8,128)}), f32[16,8,128]{2,1,0:T(8,128)S(1)}, u32[]{:S(2)}, u32[]{:S(2)}) async-start(f32[16,8,128]{2,1,0:T(8,128)} %broadcast_in_dim.61), calls=%async_computation.15 | async-start | bytes 131072 | tf_op jit(solution)/shard_map/all_to_all | solution.py:22
  278.1 11.0 %all-to-all-start.14 = ((f32[8,8,1024]{2,1,0:T(8,128)}), f32[8,8,1024]{2,1,0:T(8,128)S(1)}, u32[]{:S(2)}, u32[]{:S(2)}) async-start(f32[8,8,1024]{2,1,0:T(8,128)} %fusion.45), calls=%async_computation.14 | async-start | bytes 524288 | tf_op jit(solution)/shard_map/all_to_all | solution.py:38
  312.0 9.8 %all-to-all-start.17 = ((f32[16,8,256]{2,1,0:T(8,128)}), f32[16,8,256]{2,1,0:T(8,128)S(1)}, u32[]{:S(2)}, u32[]{:S(2)}) async-start(f32[16,8,256]{2,1,0:T(8,128)} %convolution_bitcast_fusion.1), calls=%async_computation.17 | async-start | bytes 262144 | tf_op jit(solution)/shard_map/all_to_all | solution.py:38
  322.5 9.7 %all-to-all-start.18 = ((bf16[16,8,256]{2,1,0:T(8,128)(2,1)}), bf16[16,8,256]{2,1,0:T(8,128)(2,1)S(1)}, u32[]{:S(2)}, u32[]{:S(2)}) async-start(bf16[16,8,256]{2,1,0:T(8,128)(2,1)} %broadcast_in_dim.63), calls=%async_computation.18 | async-start | bytes 131072 | tf_op jit(solution)/shard_map/all_to_all | solution.py:22
  333.4 14.2 %all-to-all-start.19 = ((bf16[8,8,4096]{2,1,0:T(8,128)(2,1)}), bf16[8,8,4096]{2,1,0:T(8,128)(2,1)S(1)}, u32[]{:S(2)}, u32[]{:S(2)}) async-start(bf16[8,8,4096]{2,1,0:T(8,128)(2,1)} %broadcast_in_dim.65), calls=%async_computation.19 | async-start | bytes 1048576 | tf_op jit(solution)/shard_map/all_to_all | solution.py:22
  348.2 10.3 %all-to-all-start.21 = ((f32[16,8,128]{2,1,0:T(8,128)}), f32[16,8,128]{2,1,0:T(8,128)S(1)}, u32[]{:S(2)}, u32[]{:S(2)}) async-start(f32[16,8,128]{2,1,0:T(8,128)} %broadcast_in_dim.67), calls=%async_computation.21 | async-start | bytes 131072 | tf_op jit(solution)/shard_map/all_to_all | solution.py:22
  358.5 11.0 %all-to-all-start.20 = ((f32[8,8,1024]{2,1,0:T(8,128)}), f32[8,8,1024]{2,1,0:T(8,128)S(1)}, u32[]{:S(2)}, u32[]{:S(2)}) async-start(f32[8,8,1024]{2,1,0:T(8,128)} %fusion.43), calls=%async_computation.20 | async-start | bytes 524288 | tf_op jit(solution)/shard_map/all_to_all | solution.py:38
  (12 other events, 199.7 us)
Sparse Core Ops, SparseCore 0:
  10.5 86.1 all-gather.1
where the time goes:
time: 416 us; the launch traced here: 413 us
  waiting for transfers between devices  128 us (31%)
  starting transfers between devices  87.5 us (21%)
  local copies, waits for them, and re-layouts  58.5 us (14%)
  matrix products  50.9 us (12%)
  blocking collectives  39.2 us (9%)
  other arithmetic  34.5 us (8%)
  between operations  14.6 us (4%)
    all_to_all x12, waiting for transfers between devices, copy_for_each(): lax.all_to_all(jnp.broadcast_to(value[None], (devices, *value.shape)), ax...  73.2 us
    all_to_all x12, starting transfers between devices, copy_for_each(): lax.all_to_all(jnp.broadcast_to(value[None], (devices, *value.shape)), ax...  51.8 us
    all_to_all x7, waiting for transfers between devices, sent_and_summed(): lax.all_to_all(cut_along(value, dim, devices), axis, 0, 0, tiled=True)  46.2 us
    all_to_all x3, blocking collectives, copy_for_each(): lax.all_to_all(jnp.broadcast_to(value[None], (devices, *value.shape)), ax...  30.2 us
    all_to_all x7, starting transfers between devices, sent_and_summed(): lax.all_to_all(cut_along(value, dim, devices), axis, 0, 0, tiled=True)  28.3 us
    dot_general x4, matrix products, body(): jnp.einsum('rhpn,rn->rhp', state, c_group, precision=lax.Precision.HIGHEST)  28.2 us
    unnamed x33, local copies, waits for them, and re-layouts  23 us
    dot_general x4, matrix products, body(): partial_value = jnp.dot(scaled, new_out, preferred_element_type=jnp.float32)  15.5 us
  transfers between devices with their start and end apart: 21, of which 19 were waited for; matrix products, arithmetic and copies ran while one was open for 17% of the time, Pallas kernels for 0%

commit v1 on v0

--- a/solution.py
+++ b/solution.py
@@ -86,7 +86,10 @@
 ):
     replica = lax.axis_index("dp")
     slot = lax.axis_index("tp")
-    traded = lax.all_to_all(zx_codes, "tp", split_axis=2, concat_axis=0, tiled=True)
+    traded = jnp.concatenate(
+        lax.all_to_all(jnp.stack(jnp.split(zx_codes, lax.axis_size("tp"), axis=2)), "tp", 0, 0),
+        axis=0,
+    )
     zx_delta = decode_pairs(traded, zx_exponents, BLK)
     row_span = traded.shape[0]
     local_cols = traded.shape[2]

time: 416 us -> 396 us (0.952)
  local copies, waits for them, and re-layouts: 58.5 us -> 40.3 us
  other arithmetic: 34.5 us -> 24.9 us
  waiting for transfers between devices: 128 us -> 136 us
    convert_element_type x1 -> x0, local copies, waits for them, and re-layouts: 11.6 us -> none  [decode_pairs(): codes.astype(jnp.float32)]
    convert_element_type x1 -> x0, other arithmetic: 8.9 us -> none  [decode_pairs(): codes.astype(jnp.float32)]
    unnamed x33 -> x45, local copies, waits for them, and re-layouts: 23 us -> 15.6 us
    all_to_all x1, waiting for transfers between devices: 8.81 us -> 14.3 us  [body(): lax.all_to_all(jnp.stack(jnp.split(zx_codes, lax.axis_size('tp'), axis=2)...]
  transfers between devices with their start and end apart: 21 -> 21, of which waited for: 19 -> 20; matrix products, arithmetic and copies ran while one was open for 17% -> 11% of each run, Pallas kernels for 0% -> 0%
where the time goes in v1:
time: 396 us; the launch traced here: 393 us
  waiting for transfers between devices  136 us (34%)
  starting transfers between devices  86.8 us (22%)
  matrix products  50.9 us (13%)
  local copies, waits for them, and re-layouts  40.3 us (10%)
  blocking collectives  39.4 us (10%)
  other arithmetic  24.9 us (6%)
  between operations  14.6 us (4%)
    all_to_all x12, waiting for transfers between devices, copy_for_each(): lax.all_to_all(jnp.broadcast_to(value[None], (devices, *value.shape)), ax...  73.9 us
    all_to_all x12, starting transfers between devices, copy_for_each(): lax.all_to_all(jnp.broadcast_to(value[None], (devices, *value.shape)), ax...  53.3 us
    all_to_all x7, waiting for transfers between devices, sent_and_summed(): lax.all_to_all(cut_along(value, dim, devices), axis, 0, 0, tiled=True)  48.3 us
    all_to_all x3, blocking collectives, copy_for_each(): lax.all_to_all(jnp.broadcast_to(value[None], (devices, *value.shape)), ax...  30.5 us
    dot_general x4, matrix products, body(): jnp.einsum('rhpn,rn->rhp', state, c_group, precision=lax.Precision.HIGHEST)  28.3 us
    all_to_all x7, starting transfers between devices, sent_and_summed(): lax.all_to_all(cut_along(value, dim, devices), axis, 0, 0, tiled=True)  26.1 us
    unnamed x45, local copies, waits for them, and re-layouts  15.6 us
    dot_general x4, matrix products, body(): partial_value = jnp.dot(scaled, new_out, preferred_element_type=jnp.float32)  15.5 us
  transfers between devices with their start and end apart: 21, of which 20 were waited for; matrix products, arithmetic and copies ran while one was open for 11% of the time, Pallas kernels for 0%

profile of v1, /device:TPU:1, one launch (start us, length us, event | category | flops | bytes accessed | tf_op | source)
XLA Modules:
  0.0 393.4 jit_solution(7191503117215772757)
XLA Ops:
  24.7 7.3 %all-to-all-start.1 = ((bf16[16,32,2,512]{3,2,1,0:T(2,128)(2,1)}), bf16[16,32,2,512]{3,2,1,0:T(2,128)(2,1)S(1)}, u32[]{:S(2)}, u32[]{:S(2)}) async-start(bf16[16,32,2,512]{3,2,1,0:T(2,128)(2,1)} %bitcast_dynamic-update-slice_fusion), calls=%async_computation.1 | async-start | bytes 2097152 | tf_op jit(solution)/shard_map/all_to_all | solution.py:90
  33.5 14.3 %all-to-all-done.1 = bf16[16,32,2,512]{3,2,1,0:T(2,128)(2,1)S(1)} async-done(((bf16[16,32,2,512]{3,2,1,0:T(2,128)(2,1)}), bf16[16,32,2,512]{3,2,1,0:T(2,128)(2,1)S(1)}, u32[]{:S(2)}, u32[]{:S(2)}) %all-to-all-start.1) | async-done | bytes 1048608 | tf_op jit(solution)/shard_map/all_to_all | solution.py:90
  48.6 7.0 %all-to-all-start = ((bf16[8,8,4096]{2,1,0:T(8,128)(2,1)}), bf16[8,8,4096]{2,1,0:T(8,128)(2,1)}, u32[]{:S(2)}, u32[]{:S(2)}) async-start(bf16[8,8,4096]{2,1,0:T(8,128)(2,1)} %broadcast_in_dim.47), calls=%async_computation | async-start | bytes 1048576 | tf_op jit(solution)/shard_map/all_to_all | solution.py:22
  66.6 6.0 %all-to-all-start.3 = ((f32[16,8,128]{2,1,0:T(8,128)}), f32[16,8,128]{2,1,0:T(8,128)S(1)}, u32[]{:S(2)}, u32[]{:S(2)}) async-start(f32[16,8,128]{2,1,0:T(8,128)} %broadcast_in_dim.49), calls=%async_computation.3 | async-start | bytes 131072 | tf_op jit(solution)/shard_map/all_to_all | solution.py:22
  84.6 8.0 %all-to-all-done.2 = f32[8,8,1024]{2,1,0:T(8,128)S(1)} async-done(((f32[8,8,1024]{2,1,0:T(8,128)}), f32[8,8,1024]{2,1,0:T(8,128)S(1)}, u32[]{:S(2)}, u32[]{:S(2)}) %all-to-all-start.2) | async-done | bytes 262176 | tf_op jit(solution)/shard_map/all_to_all | solution.py:38
  93.6 7.7 %fusion.1 = f32[8,1,8,64]{3,1,2,0:T(1,128)S(1)} fusion(f32[8,8,64,256]{3,2,1,0:T(8,128)} %param.33, f32[8,256]{1,0:T(8,128)S(1)} %get-tuple-element.17, f32[8,8,64]{2,1,0:T(8,128)S(1)} %broadcast_multiply_fusion.3, f32[8,8]{1,0:T(8,128)S(1)} %get-tuple-element.26, f32[8,256,1,1]{1,0,2,3:T(8,128)S(1)} %get-tuple-element.16), kind=kOutput, calls=%fused_computation.6 | convolution fusion | flops 15728640 | bytes 4243712 | tf_op jit(solution)/shard_map/rhpn,rn->rhp/dot_general | solution.py:145
  112.7 7.3 %fusion = bf16[4096,512]{0,1:T(8,128)(2,1)} fusion(bf16[512,4096]{1,0:T(8,128)(2,1)} %all-gather.2.cloned.1.call-done, bf16[512,4096]{1,0:T(8,128)(2,1)} %param.35), kind=kLoop, calls=%fused_computation.1 | loop fusion | flops 8388608 | bytes 12582912 | tf_op jit(solution)/shard_map/dot_general | solution.py:153
  120.0 6.5 %copy.37 = bf16[4096,512]{1,0:T(8,128)(2,1)} copy(bf16[4096,512]{0,1:T(8,128)(2,1)} %fusion) | data formatting | bytes 8388608 | tf_op jit(solution)/shard_map/dot_general | solution.py:153
  134.3 6.1 %all-to-all-done.5 = f32[16,8,256]{2,1,0:T(8,128)S(1)} async-done(((f32[16,8,256]{2,1,0:T(8,128)}), f32[16,8,256]{2,1,0:T(8,128)S(1)}, u32[]{:S(2)}, u32[]{:S(2)}) %all-to-all-start.5) | async-done | bytes 131104 | tf_op jit(solution)/shard_map/all_to_all | solution.py:38
  156.5 10.4 %all-to-all-done.7 = bf16[8,8,4096]{2,1,0:T(8,128)(2,1)S(1)} async-done(((bf16[8,8,4096]{2,1,0:T(8,128)(2,1)}), bf16[8,8,4096]{2,1,0:T(8,128)(2,1)S(1)}, u32[]{:S(2)}, u32[]{:S(2)}) %all-to-all-start.7) | async-done | bytes 524320 | tf_op jit(solution)/shard_map/all_to_all | solution.py:22
  181.5 7.3 %all-to-all-done.8 = f32[8,8,1024]{2,1,0:T(8,128)S(1)} async-done(((f32[8,8,1024]{2,1,0:T(8,128)}), f32[8,8,1024]{2,1,0:T(8,128)S(1)}, u32[]{:S(2)}, u32[]{:S(2)}) %all-to-all-start.8) | async-done | bytes 262176 | tf_op jit(solution)/shard_map/all_to_all | solution.py:38
  189.1 7.6 %fusion.11 = f32[8,1,8,64]{3,1,2,0:T(1,128)S(1)} fusion(f32[8,8,64,256]{3,2,1,0:T(8,128)} %param.33, f32[8,256]{1,0:T(8,128)S(1)} %get-tuple-element.15, f32[8,8,64]{2,1,0:T(8,128)S(1)} %broadcast_multiply_fusion.2, f32[8,8]{1,0:T(8,128)S(1)} %get-tuple-element.28, f32[8,256]{1,0:T(8,128)S(1)} %get-tuple-element.17, ...), kind=kOutput, calls=%fused_computation.21 | convolution fusion | flops 18874368 | bytes 4268544 | tf_op jit(solution)/shard_map/rhpn,rn->rhp/dot_general | solution.py:145
  197.0 10.1 %all_to_all.120 = f32[16,8,4]{1,2,0:T(4,128)S(1)} all-to-all(f32[16,8,4]{1,2,0:T(4,128)S(1)} %broadcast_in_dim.56), channel_id=1, replica_groups=mesh['dp'=8,'tp'=16] {'tp'}, dimensions={0} | all-to-all | bytes 4096 | tf_op jit(solution)/shard_map/all_to_all | solution.py:22
  215.1 6.1 %all-to-all-done.11 = f32[16,8,256]{2,1,0:T(8,128)S(1)} async-done(((f32[16,8,256]{2,1,0:T(8,128)}), f32[16,8,256]{2,1,0:T(8,128)S(1)}, u32[]{:S(2)}, u32[]{:S(2)}) %all-to-all-start.11) | async-done | bytes 131104 | tf_op jit(solution)/shard_map/all_to_all | solution.py:38
  236.6 10.4 %all-to-all-done.13 = bf16[8,8,4096]{2,1,0:T(8,128)(2,1)S(1)} async-done(((bf16[8,8,4096]{2,1,0:T(8,128)(2,1)}), bf16[8,8,4096]{2,1,0:T(8,128)(2,1)S(1)}, u32[]{:S(2)}, u32[]{:S(2)}) %all-to-all-start.13) | async-done | bytes 524320 | tf_op jit(solution)/shard_map/all_to_all | solution.py:22
  261.5 7.4 %all-to-all-done.14 = f32[8,8,1024]{2,1,0:T(8,128)S(1)} async-done(((f32[8,8,1024]{2,1,0:T(8,128)}), f32[8,8,1024]{2,1,0:T(8,128)S(1)}, u32[]{:S(2)}, u32[]{:S(2)}) %all-to-all-start.14) | async-done | bytes 262176 | tf_op jit(solution)/shard_map/all_to_all | solution.py:38
  269.2 8.0 %fusion.2 = f32[8,1,8,64]{3,1,2,0:T(1,128)S(1)} fusion(f32[8,256]{1,0:T(8,128)S(1)} %get-tuple-element.13, f32[8,8,64]{2,1,0:T(8,128)S(1)} %broadcast_multiply_fusion.1, f32[8,8]{1,0:T(8,128)S(1)} %get-tuple-element.30, f32[8,8,64,256]{3,2,1,0:T(8,128)} %param.33, f32[8,256]{1,0:T(8,128)S(1)} %get-tuple-element.15, ...), kind=kOutput, calls=%fused_computation.7 | convolution fusion | flops 22020096 | bytes 4293376 | tf_op jit(solution)/shard_map/rhpn,rn->rhp/dot_general | solution.py:145
  277.5 10.3 %all_to_all.121 = f32[16,8,4]{1,2,0:T(4,128)S(1)} all-to-all(f32[16,8,4]{1,2,0:T(4,128)S(1)} %broadcast_in_dim.62), channel_id=1, replica_groups=mesh['dp'=8,'tp'=16] {'tp'}, dimensions={0} | all-to-all | bytes 4096 | tf_op jit(solution)/shard_map/all_to_all | solution.py:22
  295.8 6.1 %all-to-all-done.17 = f32[16,8,256]{2,1,0:T(8,128)S(1)} async-done(((f32[16,8,256]{2,1,0:T(8,128)}), f32[16,8,256]{2,1,0:T(8,128)S(1)}, u32[]{:S(2)}, u32[]{:S(2)}) %all-to-all-start.17) | async-done | bytes 131104 | tf_op jit(solution)/shard_map/all_to_all | solution.py:38
  317.3 10.2 %all-to-all-done.19 = bf16[8,8,4096]{2,1,0:T(8,128)(2,1)S(1)} async-done(((bf16[8,8,4096]{2,1,0:T(8,128)(2,1)}), bf16[8,8,4096]{2,1,0:T(8,128)(2,1)S(1)}, u32[]{:S(2)}, u32[]{:S(2)}) %all-to-all-start.19) | async-done | bytes 524320 | tf_op jit(solution)/shard_map/all_to_all | solution.py:22
  342.1 7.2 %all-to-all-done.20 = f32[8,8,1024]{2,1,0:T(8,128)S(1)} async-done(((f32[8,8,1024]{2,1,0:T(8,128)}), f32[8,8,1024]{2,1,0:T(8,128)S(1)}, u32[]{:S(2)}, u32[]{:S(2)}) %all-to-all-start.20) | async-done | bytes 262176 | tf_op jit(solution)/shard_map/all_to_all | solution.py:38
  349.6 6.2 %multiply_add_fusion = f32[8,8,64,256]{3,2,1,0:T(8,128)S(1)} fusion(f32[8,256]{1,0:T(8,128)S(1)} %get-tuple-element.11, f32[8,8,64]{2,1,0:T(8,128)S(1)} %broadcast_multiply_fusion, f32[8,8]{1,0:T(8,128)S(1)} %get-tuple-element.32, f32[8,256]{1,0:T(8,128)S(1)} %get-tuple-element.13, f32[8,8,64]{2,1,0:T(8,128)S(1)} %broadcast_multiply_fusion.1, ...), kind=kLoop, calls=%fused_computation.2 | loop fusion | flops 12582912 | bytes 8487936 | tf_op jit(solution)/shard_map/add | solution.py:141
  363.1 10.2 %all_to_all.122 = f32[16,8,4]{1,2,0:T(4,128)S(1)} all-to-all(f32[16,8,4]{1,2,0:T(4,128)S(1)} %broadcast_in_dim.68), channel_id=1, replica_groups=mesh['dp'=8,'tp'=16] {'tp'}, dimensions={0} | all-to-all | bytes 4096 | tf_op jit(solution)/shard_map/all_to_all | solution.py:22
  377.0 8.9 %all_to_all.123 = f32[16,8,256]{2,1,0:T(8,128)S(1)} all-to-all(f32[16,8,256]{2,1,0:T(8,128)S(1)} %convolution_bitcast_fusion), channel_id=1, replica_groups=mesh['dp'=8,'tp'=16] {'tp'}, dimensions={0} | all-to-all | bytes 262144 | tf_op jit(solution)/shard_map/all_to_all | solution.py:38
  (217 shorter events, 182.2 us)
Async XLA Ops:
  7.2 105.5 %all-gather.2.cloned.1.call-start = ((), (), s32[]{:S(2)}) async-start(), calls=%async_computation.24 | async-start | bytes 4718592 | tf_op jit(solution)/shard_map/all_gather | solution.py:103
  10.4 45.2 %copy-start.12 = (s32[4,2,4]{2,1,0:T(2,128)S(1)}, s32[4,2,4]{2,1,0:T(2,128)}, u32[]{:S(2)}) copy-start(s32[4,2,4]{2,1,0:T(2,128)} %param.23) | copy-start | bytes 388
  24.7 23.1 %all-to-all-start.1 = ((bf16[16,32,2,512]{3,2,1,0:T(2,128)(2,1)}), bf16[16,32,2,512]{3,2,1,0:T(2,128)(2,1)S(1)}, u32[]{:S(2)}, u32[]{:S(2)}) async-start(bf16[16,32,2,512]{3,2,1,0:T(2,128)(2,1)} %bitcast_dynamic-update-slice_fusion), calls=%async_computation.1 | async-start | bytes 2097152 | tf_op jit(solution)/shard_map/all_to_all | solution.py:90
  48.6 17.3 %all-to-all-start = ((bf16[8,8,4096]{2,1,0:T(8,128)(2,1)}), bf16[8,8,4096]{2,1,0:T(8,128)(2,1)}, u32[]{:S(2)}, u32[]{:S(2)}) async-start(bf16[8,8,4096]{2,1,0:T(8,128)(2,1)} %broadcast_in_dim.47), calls=%async_computation | async-start | bytes 1048576 | tf_op jit(solution)/shard_map/all_to_all | solution.py:22
  65.2 41.4 %copy-start.13 = (f32[512]{0:T(512)S(1)}, f32[512]{0:T(512)}, u32[]{:S(2)}) copy-start(f32[512]{0:T(512)} %param.34) | copy-start | bytes 6148
  66.6 11.9 %all-to-all-start.3 = ((f32[16,8,128]{2,1,0:T(8,128)}), f32[16,8,128]{2,1,0:T(8,128)S(1)}, u32[]{:S(2)}, u32[]{:S(2)}) async-start(f32[16,8,128]{2,1,0:T(8,128)} %broadcast_in_dim.49), calls=%async_computation.3 | async-start | bytes 131072 | tf_op jit(solution)/shard_map/all_to_all | solution.py:22
  78.4 14.2 %all-to-all-start.2 = ((f32[8,8,1024]{2,1,0:T(8,128)}), f32[8,8,1024]{2,1,0:T(8,128)S(1)}, u32[]{:S(2)}, u32[]{:S(2)}) async-start(f32[8,8,1024]{2,1,0:T(8,128)} %fusion.49), calls=%async_computation.2 | async-start | bytes 524288 | tf_op jit(solution)/shard_map/all_to_all | solution.py:38
  102.2 10.3 %all-to-all-start.4 = ((f32[16,8,4]{1,2,0:T(4,128)}), f32[16,8,4]{1,2,0:T(4,128)S(1)}, u32[]{:S(2)}, u32[]{:S(2)}) async-start(f32[16,8,4]{1,2,0:T(4,128)} %broadcast_in_dim.50), calls=%async_computation.4 | async-start | bytes 65536 | tf_op jit(solution)/shard_map/all_to_all | solution.py:22
  130.5 50.8 %copy-start.11 = (f32[8]{0:T(128)S(1)}, f32[8]{0:T(128)}, u32[]{:S(2)}) copy-start(f32[8]{0:T(128)} %param.28) | copy-start | bytes 100
  130.5 10.0 %all-to-all-start.5 = ((f32[16,8,256]{2,1,0:T(8,128)}), f32[16,8,256]{2,1,0:T(8,128)S(1)}, u32[]{:S(2)}, u32[]{:S(2)}) async-start(f32[16,8,256]{2,1,0:T(8,128)} %convolution_bitcast_fusion.3), calls=%async_computation.5 | async-start | bytes 262144 | tf_op jit(solution)/shard_map/all_to_all | solution.py:38
  141.1 9.7 %all-to-all-start.6 = ((bf16[16,8,256]{2,1,0:T(8,128)(2,1)}), bf16[16,8,256]{2,1,0:T(8,128)(2,1)S(1)}, u32[]{:S(2)}, u32[]{:S(2)}) async-start(bf16[16,8,256]{2,1,0:T(8,128)(2,1)} %broadcast_in_dim.51), calls=%async_computation.6 | async-start | bytes 131072 | tf_op jit(solution)/shard_map/all_to_all | solution.py:22
  152.0 14.9 %all-to-all-start.7 = ((bf16[8,8,4096]{2,1,0:T(8,128)(2,1)}), bf16[8,8,4096]{2,1,0:T(8,128)(2,1)S(1)}, u32[]{:S(2)}, u32[]{:S(2)}) async-start(bf16[8,8,4096]{2,1,0:T(8,128)(2,1)} %broadcast_in_dim.53), calls=%async_computation.7 | async-start | bytes 1048576 | tf_op jit(solution)/shard_map/all_to_all | solution.py:22
  167.6 10.3 %all-to-all-start.9 = ((f32[16,8,128]{2,1,0:T(8,128)}), f32[16,8,128]{2,1,0:T(8,128)S(1)}, u32[]{:S(2)}, u32[]{:S(2)}) async-start(f32[16,8,128]{2,1,0:T(8,128)} %broadcast_in_dim.55), calls=%async_computation.9 | async-start | bytes 131072 | tf_op jit(solution)/shard_map/all_to_all | solution.py:22
  177.9 10.9 %all-to-all-start.8 = ((f32[8,8,1024]{2,1,0:T(8,128)}), f32[8,8,1024]{2,1,0:T(8,128)S(1)}, u32[]{:S(2)}, u32[]{:S(2)}) async-start(f32[8,8,1024]{2,1,0:T(8,128)} %fusion.47), calls=%async_computation.8 | async-start | bytes 524288 | tf_op jit(solution)/shard_map/all_to_all | solution.py:38
  211.4 9.8 %all-to-all-start.11 = ((f32[16,8,256]{2,1,0:T(8,128)}), f32[16,8,256]{2,1,0:T(8,128)S(1)}, u32[]{:S(2)}, u32[]{:S(2)}) async-start(f32[16,8,256]{2,1,0:T(8,128)} %convolution_bitcast_fusion.2), calls=%async_computation.11 | async-start | bytes 262144 | tf_op jit(solution)/shard_map/all_to_all | solution.py:38
  221.9 9.7 %all-to-all-start.12 = ((bf16[16,8,256]{2,1,0:T(8,128)(2,1)}), bf16[16,8,256]{2,1,0:T(8,128)(2,1)S(1)}, u32[]{:S(2)}, u32[]{:S(2)}) async-start(bf16[16,8,256]{2,1,0:T(8,128)(2,1)} %broadcast_in_dim.57), calls=%async_computation.12 | async-start | bytes 131072 | tf_op jit(solution)/shard_map/all_to_all | solution.py:22
  232.8 14.2 %all-to-all-start.13 = ((bf16[8,8,4096]{2,1,0:T(8,128)(2,1)}), bf16[8,8,4096]{2,1,0:T(8,128)(2,1)S(1)}, u32[]{:S(2)}, u32[]{:S(2)}) async-start(bf16[8,8,4096]{2,1,0:T(8,128)(2,1)} %broadcast_in_dim.59), calls=%async_computation.13 | async-start | bytes 1048576 | tf_op jit(solution)/shard_map/all_to_all | solution.py:22
  247.7 10.3 %all-to-all-start.15 = ((f32[16,8,128]{2,1,0:T(8,128)}), f32[16,8,128]{2,1,0:T(8,128)S(1)}, u32[]{:S(2)}, u32[]{:S(2)}) async-start(f32[16,8,128]{2,1,0:T(8,128)} %broadcast_in_dim.61), calls=%async_computation.15 | async-start | bytes 131072 | tf_op jit(solution)/shard_map/all_to_all | solution.py:22
  257.9 11.0 %all-to-all-start.14 = ((f32[8,8,1024]{2,1,0:T(8,128)}), f32[8,8,1024]{2,1,0:T(8,128)S(1)}, u32[]{:S(2)}, u32[]{:S(2)}) async-start(f32[8,8,1024]{2,1,0:T(8,128)} %fusion.45), calls=%async_computation.14 | async-start | bytes 524288 | tf_op jit(solution)/shard_map/all_to_all | solution.py:38
  292.1 9.8 %all-to-all-start.17 = ((f32[16,8,256]{2,1,0:T(8,128)}), f32[16,8,256]{2,1,0:T(8,128)S(1)}, u32[]{:S(2)}, u32[]{:S(2)}) async-start(f32[16,8,256]{2,1,0:T(8,128)} %convolution_bitcast_fusion.1), calls=%async_computation.17 | async-start | bytes 262144 | tf_op jit(solution)/shard_map/all_to_all | solution.py:38
  302.6 9.7 %all-to-all-start.18 = ((bf16[16,8,256]{2,1,0:T(8,128)(2,1)}), bf16[16,8,256]{2,1,0:T(8,128)(2,1)S(1)}, u32[]{:S(2)}, u32[]{:S(2)}) async-start(bf16[16,8,256]{2,1,0:T(8,128)(2,1)} %broadcast_in_dim.63), calls=%async_computation.18 | async-start | bytes 131072 | tf_op jit(solution)/shard_map/all_to_all | solution.py:22
  313.5 14.0 %all-to-all-start.19 = ((bf16[8,8,4096]{2,1,0:T(8,128)(2,1)}), bf16[8,8,4096]{2,1,0:T(8,128)(2,1)S(1)}, u32[]{:S(2)}, u32[]{:S(2)}) async-start(bf16[8,8,4096]{2,1,0:T(8,128)(2,1)} %broadcast_in_dim.65), calls=%async_computation.19 | async-start | bytes 1048576 | tf_op jit(solution)/shard_map/all_to_all | solution.py:22
  328.2 10.3 %all-to-all-start.21 = ((f32[16,8,128]{2,1,0:T(8,128)}), f32[16,8,128]{2,1,0:T(8,128)S(1)}, u32[]{:S(2)}, u32[]{:S(2)}) async-start(f32[16,8,128]{2,1,0:T(8,128)} %broadcast_in_dim.67), calls=%async_computation.21 | async-start | bytes 131072 | tf_op jit(solution)/shard_map/all_to_all | solution.py:22
  338.5 10.8 %all-to-all-start.20 = ((f32[8,8,1024]{2,1,0:T(8,128)}), f32[8,8,1024]{2,1,0:T(8,128)S(1)}, u32[]{:S(2)}, u32[]{:S(2)}) async-start(f32[8,8,1024]{2,1,0:T(8,128)} %fusion.43), calls=%async_computation.20 | async-start | bytes 524288 | tf_op jit(solution)/shard_map/all_to_all | solution.py:38
  (12 other events, 268.6 us)
Sparse Core Ops, SparseCore 0:
  10.6 86.6 all-gather.1
